TPU v7x, 32 devices: a whole 2x2x4 slice. The times are simulated.
32 devices in a mesh: rep: 2 (over x), shard: 16 (over z, y, core).
Axes of the slice: x: 2, y: 2, z: 4, core: 2. Of those that a mesh axis runs over, the one named last changes fastest.
Arguments:
- tokens: bfloat16 [4096, 2048], P(('rep', 'shard')), may hold values from -6 to 6
- segment_ids: int32 [4096], P(('rep', 'shard')), may hold values from -1 to 31, as said below
- cotangent: bfloat16 [4096, 2048], P(('rep', 'shard')), may hold values from -6 to 6
- w_qkv: bfloat16 [2048, 6144], P('shard'), may hold values from -0.125 to 0.125
- w_out: bfloat16 [2048, 2048], P('shard'), may hold values from -0.125 to 0.125
- w_gate_up: bfloat16 [2048, 16384], P('shard'), may hold values from -0.125 to 0.125
- w_down: bfloat16 [8192, 2048], P('shard'), may hold values from -0.0625 to 0.0625
- q_gain: bfloat16 [2048], P('shard'), may hold values from 0.5 to 1.5
- k_gain: bfloat16 [2048], P('shard'), may hold values from 0.5 to 1.5
- attn_gain: bfloat16 [2048], P('shard'), may hold values from 0.5 to 1.5
- mlp_gain: bfloat16 [2048], P('shard'), may hold values from 0.5 to 1.5
Outputs:
- output: bfloat16 [4096, 2048], P(('rep', 'shard'))
- grad_tokens: float32 [4096, 2048], P(('rep', 'shard'))
- grad_qkv: float32 [2048, 6144], P('shard')
- grad_out: float32 [2048, 2048], P('shard')
- grad_gate_up: float32 [2048, 16384], P('shard')
- grad_down: float32 [8192, 2048], P('shard')
- grad_q_gain: float32 [2048], P('shard')
- grad_k_gain: float32 [2048], P('shard')
- grad_attn_gain: float32 [2048], P('shard')
- grad_mlp_gain: float32 [2048], P('shard')
Inputs may be any that keep to these rules, and one draw needn't show every extreme that they name: `segment_ids`: within each block of 128 slots, live slots come first in runs of equal ids numbered upwards from 0 (one packed sequence each), each run starting at a slot whose index within the block is a multiple of 4, then padding slots with id -1; at least one block has no padding and starts a run at every multiple of 4.
All inputs are finite; a program needn't handle non-finite values.
Results may differ from a plain program's by a relative error of at most 0.02.
Values may be sent and summed in bfloat16 or wider, within the bound.
A program may use at most 384 MiB of HBM per device.

v0:
```python
import jax
import jax.numpy as jnp
from jax import lax
from jax.sharding import PartitionSpec as P

H = 16
EPSILON = 1e-06
THETA = 500000.0


def positions(seg_row):
    count = seg_row.shape[0]
    slots = jnp.arange(count, dtype=jnp.int32)
    starts = jnp.concatenate([jnp.ones((1,), jnp.bool_), seg_row[1:] != seg_row[:-1]])
    first = lax.cummax(jnp.where(starts, slots, 0), axis=0)
    return slots - first


def rope_tables(seg_row, head_width):
    half_width = head_width // 2
    spots = positions(seg_row).astype(jnp.float32)
    inverse = THETA ** (-(2.0 * jnp.arange(half_width, dtype=jnp.float32)) / head_width)
    angle = spots[:, None] * inverse[None, :]
    return (jnp.cos(angle), jnp.sin(angle))


def rotate(matrix, cosine, sine, num_heads):
    count, width = matrix.shape
    shaped = matrix.reshape(count, num_heads, width // num_heads)
    half_width = shaped.shape[2] // 2
    first_half = shaped[..., :half_width]
    second_half = shaped[..., half_width:]
    cos_head = cosine[:, None, :]
    sin_head = sine[:, None, :]
    joined = jnp.concatenate(
        [
            first_half * cos_head - second_half * sin_head,
            second_half * cos_head + first_half * sin_head,
        ],
        axis=-1,
    )
    return joined.reshape(count, width)


def allowed(seg_row):
    count = seg_row.shape[0]
    slots = jnp.arange(count)
    return (seg_row[:, None] == seg_row[None, :]) & (slots[None, :] <= slots[:, None])


def norm_forward(vector, gain):
    rscale = lax.rsqrt(jnp.mean(vector * vector, axis=-1, keepdims=True) + EPSILON)
    normed = vector * rscale
    return (normed * gain, normed, rscale)


def norm_backward(upstream, normed, rscale, gain):
    scaled = upstream * gain
    inner = jnp.mean(scaled * normed, axis=-1, keepdims=True)
    return (rscale * (scaled - normed * inner), jnp.sum(upstream * normed, axis=0))


def contract_last(left, right):
    return lax.dot_general(
        left, right, (((1,), (1,)), ((), ())), preferred_element_type=jnp.float32
    )


def contract_first(left, right):
    return lax.dot_general(
        left, right, (((0,), (0,)), ((), ())), preferred_element_type=jnp.float32
    )


def head_split(matrix, num_heads):
    return matrix.reshape(matrix.shape[0], num_heads, -1)


def attention_scores(query_rot, keys_rot, seg_row, num_heads):
    head_width = query_rot.shape[1] // num_heads
    scores = jnp.einsum(
        "thd,shd->hts",
        head_split(query_rot, num_heads),
        head_split(keys_rot, num_heads),
        preferred_element_type=jnp.float32,
    ) * head_width ** (-0.5)
    return jnp.where(allowed(seg_row)[None], scores, -1e30)


def attention_forward(query_rot, keys_rot, values_b, seg_row, num_heads):
    scores = attention_scores(query_rot, keys_rot, seg_row, num_heads)
    top = jnp.max(scores, axis=-1, keepdims=True)
    log_total = top[..., 0] + jnp.log(jnp.sum(jnp.exp(scores - top), axis=-1))
    probs_b = jnp.exp(scores - log_total[..., None]).astype(jnp.bfloat16)
    context = jnp.einsum(
        "hts,shd->thd", probs_b, head_split(values_b, num_heads), preferred_element_type=jnp.float32
    )
    return (context.reshape(query_rot.shape), log_total)


def attention_backward(
    query_rot, keys_rot, values_b, seg_row, log_total, context, d_context_b, num_heads
):
    count, width = query_rot.shape
    head_width = width // num_heads
    scores = attention_scores(query_rot, keys_rot, seg_row, num_heads)
    probs = jnp.exp(scores - log_total[..., None])
    probs_b = probs.astype(jnp.bfloat16)
    d_heads = head_split(d_context_b, num_heads)
    d_values = jnp.einsum("hts,thd->shd", probs_b, d_heads, preferred_element_type=jnp.float32)
    d_probs = jnp.einsum(
        "thd,shd->hts", d_heads, head_split(values_b, num_heads), preferred_element_type=jnp.float32
    )
    delta = jnp.sum(
        d_heads.astype(jnp.float32) * context.reshape(count, num_heads, head_width), axis=-1
    ).T
    d_scores_b = (probs * (d_probs - delta[..., None]) * head_width ** (-0.5)).astype(jnp.bfloat16)
    d_query = jnp.einsum(
        "hts,shd->thd",
        d_scores_b,
        head_split(keys_rot, num_heads),
        preferred_element_type=jnp.float32,
    )
    d_keys = jnp.einsum(
        "hts,thd->shd",
        d_scores_b,
        head_split(query_rot, num_heads),
        preferred_element_type=jnp.float32,
    )
    return (
        d_query.reshape(count, width),
        d_keys.reshape(count, width),
        d_values.reshape(count, width),
    )


def add_block(left, weight_rows):
    return jnp.dot(left, weight_rows, preferred_element_type=jnp.float32)


def fold_gain(left, pieces):
    weight_rows, gain_piece = pieces
    return (add_block(left, weight_rows), gain_piece)


def fold_two_gains(left, pieces):
    weight_rows, first_piece, second_piece = pieces
    return (add_block(left, weight_rows), first_piece, second_piece)


def back_rows(upstream, piece):
    return contract_last(upstream, piece)


def fold_owned(left_rows, upstream_piece):
    return contract_first(left_rows, upstream_piece)


def fold_all_owned(lefts, pieces):
    return tuple((fold_owned(left_rows, piece) for left_rows, piece in zip(lefts, pieces)))


def shards(
    tokens,
    segment_ids,
    cotangent,
    w_qkv,
    w_out,
    w_gate_up,
    w_down,
    q_gain,
    k_gain,
    attn_gain,
    mlp_gain,
):
    count, width = tokens.shape
    ff_width = w_gate_up.shape[1] // 2
    num_heads = H
    cosine, sine = rope_tables(segment_ids, width // num_heads)
    qkv, query_gain_full, keys_gain_full = fold_two_gains(
        tokens,
        (
            lax.all_gather(w_qkv, "shard", axis=0, tiled=True),
            lax.all_gather(q_gain, "shard", axis=0, tiled=True),
            lax.all_gather(k_gain, "shard", axis=0, tiled=True),
        ),
    )
    gain_query = query_gain_full.astype(jnp.float32)
    gain_keys = keys_gain_full.astype(jnp.float32)
    query_norm, query_hat, query_scale = norm_forward(qkv[:, :width], gain_query)
    keys_norm, keys_hat, keys_scale = norm_forward(qkv[:, width : 2 * width], gain_keys)
    query_rot = rotate(query_norm, cosine, sine, num_heads).astype(jnp.bfloat16)
    keys_rot = rotate(keys_norm, cosine, sine, num_heads).astype(jnp.bfloat16)
    values_b = qkv[:, 2 * width :].astype(jnp.bfloat16)
    context, log_total = attention_forward(query_rot, keys_rot, values_b, segment_ids, num_heads)
    context_b = context.astype(jnp.bfloat16)
    attn_raw, attn_gain_full = fold_gain(
        context_b,
        (
            lax.all_gather(w_out, "shard", axis=0, tiled=True),
            lax.all_gather(attn_gain, "shard", axis=0, tiled=True),
        ),
    )
    gain_attn = attn_gain_full.astype(jnp.float32)
    attn_norm, attn_hat, attn_scale = norm_forward(attn_raw, gain_attn)
    resid = tokens.astype(jnp.float32) + attn_norm
    resid_b = resid.astype(jnp.bfloat16)
    gate_up, mlp_gain_full = fold_gain(
        resid_b,
        (
            lax.all_gather(w_gate_up, "shard", axis=0, tiled=True),
            lax.all_gather(mlp_gain, "shard", axis=0, tiled=True),
        ),
    )
    gain_mlp = mlp_gain_full.astype(jnp.float32)
    gate_raw = gate_up[:, :ff_width]
    up_raw = gate_up[:, ff_width:]
    sigma = jax.nn.sigmoid(gate_raw)
    activated = gate_raw * sigma
    mixed_b = (activated * up_raw).astype(jnp.bfloat16)
    down_raw = add_block(mixed_b, lax.all_gather(w_down, "shard", axis=0, tiled=True))
    down_norm, down_hat, down_scale = norm_forward(down_raw, gain_mlp)
    output = (resid + down_norm).astype(jnp.bfloat16)
    valid = (segment_ids >= 0).astype(jnp.float32)[:, None]
    d_out = cotangent.astype(jnp.float32) * valid
    d_down, grad_mlp = norm_backward(d_out, down_hat, down_scale, gain_mlp)
    d_down_b = d_down.astype(jnp.bfloat16)
    d_mixed = back_rows(d_down_b, lax.all_gather(w_down, "shard", axis=0, tiled=True))
    d_gate = d_mixed * up_raw * sigma * (1.0 + gate_raw * (1.0 - sigma))
    d_up = d_mixed * activated
    d_gu_b = jnp.concatenate([d_gate, d_up], axis=1).astype(jnp.bfloat16)
    d_resid = d_out + back_rows(d_gu_b, lax.all_gather(w_gate_up, "shard", axis=0, tiled=True))
    d_attn, grad_attn = norm_backward(d_resid, attn_hat, attn_scale, gain_attn)
    d_attn_b = d_attn.astype(jnp.bfloat16)
    out_full, qkv_full = (
        lax.all_gather(w_out, "shard", axis=0, tiled=True),
        lax.all_gather(w_qkv, "shard", axis=0, tiled=True),
    )
    d_context_b = contract_last(d_attn_b, out_full).astype(jnp.bfloat16)
    d_query_rot, d_keys_rot, d_values = attention_backward(
        query_rot, keys_rot, values_b, segment_ids, log_total, context, d_context_b, num_heads
    )
    d_query_norm = rotate(d_query_rot, cosine, -sine, num_heads)
    d_keys_norm = rotate(d_keys_rot, cosine, -sine, num_heads)
    d_query, grad_query = norm_backward(d_query_norm, query_hat, query_scale, gain_query)
    d_keys, grad_keys = norm_backward(d_keys_norm, keys_hat, keys_scale, gain_keys)
    d_qkv_b = jnp.concatenate([d_query, d_keys, d_values], axis=1).astype(jnp.bfloat16)
    grad_tokens = d_resid + contract_last(d_qkv_b, qkv_full)
    mixed_rows, resid_rows, token_rows, context_rows = (
        lax.all_to_all(mixed_b, "shard", split_axis=1, concat_axis=0, tiled=True),
        lax.all_to_all(resid_b, "shard", split_axis=1, concat_axis=0, tiled=True),
        lax.all_to_all(tokens, "shard", split_axis=1, concat_axis=0, tiled=True),
        lax.all_to_all(context_b, "shard", split_axis=1, concat_axis=0, tiled=True),
    )
    grad_down, grad_gate_up, grad_qkv_own, grad_out_own = fold_all_owned(
        (mixed_rows, resid_rows, token_rows, context_rows),
        (
            lax.all_gather(d_down_b, "shard", axis=0, tiled=True),
            lax.all_gather(d_gu_b, "shard", axis=0, tiled=True),
            lax.all_gather(d_qkv_b, "shard", axis=0, tiled=True),
            lax.all_gather(d_attn_b, "shard", axis=0, tiled=True),
        ),
    )
    gains_own = (
        lax.psum_scatter(
            grad_query.astype(jnp.bfloat16), "shard", scatter_dimension=0, tiled=True
        ).astype(jnp.float32),
        lax.psum_scatter(
            grad_keys.astype(jnp.bfloat16), "shard", scatter_dimension=0, tiled=True
        ).astype(jnp.float32),
        lax.psum_scatter(
            grad_attn.astype(jnp.bfloat16), "shard", scatter_dimension=0, tiled=True
        ).astype(jnp.float32),
        lax.psum_scatter(
            grad_mlp.astype(jnp.bfloat16), "shard", scatter_dimension=0, tiled=True
        ).astype(jnp.float32),
    )
    summed = (
        lax.psum(grad_qkv_own.astype(jnp.bfloat16), "rep").astype(jnp.float32),
        lax.psum(grad_out_own.astype(jnp.bfloat16), "rep").astype(jnp.float32),
        lax.psum(grad_gate_up.astype(jnp.bfloat16), "rep").astype(jnp.float32),
        lax.psum(grad_down.astype(jnp.bfloat16), "rep").astype(jnp.float32),
        lax.psum(gains_own[0].astype(jnp.bfloat16), "rep").astype(jnp.float32),
        lax.psum(gains_own[1].astype(jnp.bfloat16), "rep").astype(jnp.float32),
        lax.psum(gains_own[2].astype(jnp.bfloat16), "rep").astype(jnp.float32),
        lax.psum(gains_own[3].astype(jnp.bfloat16), "rep").astype(jnp.float32),
    )
    grad_qkv, grad_out, grad_gu, grad_dn, grad_q, grad_k, grad_a, grad_m = summed
    return (
        output,
        grad_tokens,
        grad_qkv,
        grad_out,
        grad_gu,
        grad_dn,
        grad_q,
        grad_k,
        grad_a,
        grad_m,
    )


def solution(mesh):
    return jax.shard_map(
        shards,
        mesh=mesh,
        in_specs=(
            P(("rep", "shard"), None),
            P(("rep", "shard")),
            P(("rep", "shard"), None),
            P("shard", None),
            P("shard", None),
            P("shard", None),
            P("shard", None),
            P("shard"),
            P("shard"),
            P("shard"),
            P("shard"),
        ),
        out_specs=(
            P(("rep", "shard"), None),
            P(("rep", "shard"), None),
            P("shard", None),
            P("shard", None),
            P("shard", None),
            P("shard", None),
            P("shard"),
            P("shard"),
            P("shard"),
            P("shard"),
        ),
        check_vma=False,
    )
```

profile of v0, /device:TPU:0, one launch (start us, length us, event | category | flops | bytes accessed | tf_op | source)
XLA Modules:
  0.0 1692.7 jit_solution(17944830758551619071)
XLA Ops:
  10.1 23.4 %all-gather = bf16[16,1,128]{2,1,0:T(2,128)(2,1)S(1)} all-gather(bf16[1,1,128]{2,1,0:T(2,128)(2,1)S(1)} %bitcast.143), channel_id=1, replica_groups=mesh['rep'=2,'shard'=16] {'shard'}, dimensions={0}, use_global_device_ids=true | all-gather | bytes 4352 | tf_op jit(solution)/shard_map/all_gather | solution.py:184
  33.5 18.0 %all-gather.1 = bf16[16,1,128]{2,1,0:T(2,128)(2,1)S(1)} all-gather(bf16[1,1,128]{2,1,0:T(2,128)(2,1)S(1)} %bitcast.144), channel_id=1, replica_groups=mesh['rep'=2,'shard'=16] {'shard'}, dimensions={0}, use_global_device_ids=true | all-gather | bytes 4352 | tf_op jit(solution)/shard_map/all_gather | solution.py:185
  51.8 19.3 %all-gather.2 = bf16[16,1,128]{2,1,0:T(2,128)(2,1)S(1)} all-gather(bf16[1,1,128]{2,1,0:T(2,128)(2,1)S(1)} %bitcast.145), channel_id=1, replica_groups=mesh['rep'=2,'shard'=16] {'shard'}, dimensions={0}, use_global_device_ids=true | all-gather | bytes 4352 | tf_op jit(solution)/shard_map/all_gather | solution.py:201
  71.2 18.0 %all-gather.3 = bf16[16,1,128]{2,1,0:T(2,128)(2,1)S(1)} all-gather(bf16[1,1,128]{2,1,0:T(2,128)(2,1)S(1)} %bitcast.146), channel_id=1, replica_groups=mesh['rep'=2,'shard'=16] {'shard'}, dimensions={0}, use_global_device_ids=true | all-gather | bytes 4352 | tf_op jit(solution)/shard_map/all_gather | solution.py:212
  89.9 51.1 %all-gather.13.cloned.1.call-done = bf16[2048,6144]{1,0:T(8,128)(2,1)} async-done(((bf16[128,6144]{1,0:T(8,128)(2,1)}), bf16[2048,6144]{1,0:T(8,128)(2,1)}) %all-gather.13.cloned.1.call-update) | async-done | bytes 25165840 | tf_op jit(solution)/shard_map/all_gather | solution.py:183
  158.2 59.4 %all-gather.15.cloned.1.call-done = bf16[2048,2048]{1,0:T(8,128)(2,1)} async-done(((bf16[128,2048]{1,0:T(8,128)(2,1)}), bf16[2048,2048]{1,0:T(8,128)(2,1)}) %all-gather.15.cloned.1.call-update) | async-done | bytes 8388624 | tf_op jit(solution)/shard_map/all_gather | solution.py:200
  224.6 319.3 %all-gather.17.cloned.1.call-done = bf16[2048,16384]{1,0:T(8,128)(2,1)} async-done(((bf16[128,16384]{1,0:T(8,128)(2,1)}), bf16[2048,16384]{1,0:T(8,128)(2,1)}) %all-gather.17.cloned.1.call-update) | async-done | bytes 67108880 | tf_op jit(solution)/shard_map/all_gather | solution.py:211
  544.0 29.4 %fusion.28 = f32[128,16384]{1,0:T(8,128)} fusion(bf16[128,2048]{1,0:T(8,128)(2,1)} %fusion.10, bf16[2048,16384]{1,0:T(8,128)(2,1)} %all-gather.17.cloned.1.call-done), kind=kOutput, calls=%fused_computation.105 | convolution fusion | flops 8589934592 | bytes 76021760 | tf_op jit(solution)/shard_map/dot_general | solution.py:138
  579.3 134.2 %all-gather.19.cloned.1.call-done = bf16[8192,2048]{1,0:T(8,128)(2,1)} async-done(((bf16[512,2048]{1,0:T(8,128)(2,1)}), bf16[8192,2048]{1,0:T(8,128)(2,1)}) %all-gather.19.cloned.1.call-update) | async-done | bytes 33554448 | tf_op jit(solution)/shard_map/all_gather | solution.py:221
  713.5 13.6 multiply_reduce_fusion.7
  729.3 20.1 %multiply_convert_fusion.1 = (bf16[128,8192]{1,0:T(8,128)(2,1)}, bf16[128,8192]{1,0:T(8,128)(2,1)}) fusion(f32[128,16384]{1,0:T(8,128)} %fusion.28, bf16[128,2048]{1,0:T(8,128)(2,1)} %multiply_convert_fusion.6, bf16[8192,2048]{1,0:T(8,128)(2,1)} %all-gather.19.cloned.1.call-done), kind=kOutput, calls=%fused_computation.5 | convolution fusion | flops 4308598784 | bytes 46661632 | tf_op jit(solution)/shard_map/dot_general | solution.py:64
  749.4 30.4 %multiply_reduce_fusion.1 = (bf16[2048]{0:T(1024)(128)(2,1)S(1)}, f32[128]{0:T(128)S(1)}, f32[128,2048]{1,0:T(8,128)}) fusion(f32[128,2048]{1,0:T(8,128)} %copy-done.2, f32[128]{0:T(128)S(1)} %add_rsqrt_fusion.1, f32[2048]{0:T(1024)S(1)} %bitcast.131, bf16[2048,16384]{1,0:T(8,128)(2,1)} %all-gather.17.cloned.1.call-done, ...), kind=kOutput, calls=%fused_computation.36 | convolution fusion | flops 8600680448 | bytes 73938432 | tf_op jit(solution)/shard_map/dot_general | solution.py:64
  813.0 27.7 %all_to_all.73 = bf16[128,16,128]{0,2,1:T(8,128)(2,1)} all-to-all(bf16[128,16,128]{0,2,1:T(8,128)(2,1)S(1)} %bitcast.127), channel_id=1, replica_groups=mesh['rep'=2,'shard'=16] {'shard'}, dimensions={1} | all-to-all | bytes 1048576 | tf_op jit(solution)/shard_map/all_to_all | solution.py:252
  852.0 20.5 %all-to-all-done.1 = bf16[128,16,128]{0,2,1:T(8,128)(2,1)S(1)} async-done(((bf16[128,16,128]{0,2,1:T(8,128)(2,1)}), bf16[128,16,128]{0,2,1:T(8,128)(2,1)S(1)}, u32[]{:S(2)}, u32[]{:S(2)}) %all-to-all-start.1) | async-done | bytes 524320 | tf_op jit(solution)/shard_map/all_to_all | solution.py:253
  885.5 50.8 %all-to-all-done.3 = bf16[128,16,512]{2,0,1:T(8,128)(2,1)} async-done(((bf16[128,16,512]{2,0,1:T(8,128)(2,1)}), bf16[128,16,512]{2,0,1:T(8,128)(2,1)}, u32[]{:S(2)}, u32[]{:S(2)}) %all-to-all-start.3) | async-done | bytes 2097184 | tf_op jit(solution)/shard_map/all_to_all | solution.py:250
  936.3 19.3 %all-to-all-start.2 = ((bf16[128,16,128]{2,0,1:T(8,128)(2,1)}), bf16[128,16,128]{2,0,1:T(8,128)(2,1)S(1)}, u32[]{:S(2)}, u32[]{:S(2)}) async-start(bf16[128,16,128]{2,0,1:T(8,128)(2,1)} %copy_bitcast_fusion.1), calls=%async_computation.2 | async-start | bytes 1048576 | tf_op jit(solution)/shard_map/all_to_all | solution.py:251
  956.1 35.1 %all-gather.27.cloned.1.call-done = bf16[2048,2048]{1,0:T(8,128)(2,1)} async-done(((bf16[128,2048]{1,0:T(8,128)(2,1)}), bf16[2048,2048]{1,0:T(8,128)(2,1)}) %all-gather.27.cloned.1.call-update) | async-done | bytes 8388624 | tf_op jit(solution)/shard_map/all_gather | solution.py:258
  1001.1 119.8 %all-gather.21.cloned.1.call-done = bf16[2048,6144]{1,0:T(8,128)(2,1)} async-done(((bf16[128,6144]{1,0:T(8,128)(2,1)}), bf16[2048,6144]{1,0:T(8,128)(2,1)}) %all-gather.21.cloned.1.call-update) | async-done | bytes 25165840 | tf_op jit(solution)/shard_map/all_gather | solution.py:260
  1120.9 12.9 fusion
  1133.8 315.4 %all-gather.25.cloned.1.call-done = bf16[2048,16384]{1,0:T(8,128)(2,1)} async-done(((bf16[128,16384]{1,0:T(8,128)(2,1)}), bf16[2048,16384]{1,0:T(8,128)(2,1)}) %all-gather.25.cloned.1.call-update) | async-done | bytes 67108880 | tf_op jit(solution)/shard_map/all_gather | solution.py:259
  1449.2 26.2 %convolution_convert_fusion = bf16[128,16384]{1,0:T(8,128)(2,1)} fusion(bf16[2048,128]{1,0:T(8,128)(2,1)S(1)} %bitcast.124, bf16[2048,16384]{1,0:T(8,128)(2,1)} %all-gather.25.cloned.1.call-done), kind=kOutput, calls=%fused_computation | convolution fusion | flops 8592031744 | bytes 71827456 | tf_op jit(solution)/shard_map/dot_general | solution.py:70
  1477.2 60.7 %all-reduce.4 = (bf16[2048]{0:T(1024)(128)(2,1)S(1)}, bf16[2048]{0:T(1024)(128)(2,1)S(1)}, bf16[2048]{0:T(1024)(128)(2,1)S(1)}, bf16[2048]{0:T(1024)(128)(2,1)S(1)}) all-reduce(bf16[2048]{0:T(1024)(128)(2,1)S(1)} %get-tuple-element.55, ...), channel_id=2, replica_groups=mesh['rep'=2,'shard'=16] {'shard'}, use_global_device_ids=true, to_apply=%region_17.18.clone | all-reduce | flops 8192 | bytes 32768
  1545.6 14.4 convolution_add_fusion
  1560.0 113.7 %all-reduce.9.cloned.1.call-done = (bf16[128,6144]{0,1:T(8,128)(2,1)}, bf16[128,2048]{1,0:T(8,128)(2,1)}, bf16[128,16384]{1,0:T(8,128)(2,1)}, bf16[512,2048]{1,0:T(8,128)(2,1)}) async-done(((bf16[128,6144]{0,1:T(8,128)(2,1)}, bf16[128,2048]{1,0:T(8,128)(2,1)}, bf16[128,16384]{1,0:T(8,128)(2,1)}, bf16[512,2048]{1,0:T(8,128)(2,1)}), (bf16[128,6144]{0,1:T(8,128)(2,1)}, bf16[128,2048]{1,0:T(8,128)(2,1)}, ...) | async-done | bytes 8388624 | tf_op jit(solution)/shard_map/psum | solution.py:279
  (163 shorter events, 124.8 us)
Async XLA Ops:
  7.2 26.3 %copy-start.30 = (bf16[128]{0:T(256)(128)(2,1)S(1)}, bf16[128]{0:T(256)(128)(2,1)}, u32[]{:S(2)}) copy-start(bf16[128]{0:T(256)(128)(2,1)} %param.19) | copy-start | bytes 772
  7.2 44.3 %copy-start.28 = (s32[128]{0:T(128)S(1)}, s32[128]{0:T(128)}, u32[]{:S(2)}) copy-start(s32[128]{0:T(128)} %param.12) | copy-start | bytes 1540
  7.2 44.6 %copy-start.31 = (bf16[128]{0:T(256)(128)(2,1)S(1)}, bf16[128]{0:T(256)(128)(2,1)}, u32[]{:S(2)}) copy-start(bf16[128]{0:T(256)(128)(2,1)} %param.20) | copy-start | bytes 772
  7.2 63.9 %copy-start.32 = (bf16[128]{0:T(256)(128)(2,1)S(1)}, bf16[128]{0:T(256)(128)(2,1)}, u32[]{:S(2)}) copy-start(bf16[128]{0:T(256)(128)(2,1)} %param.21) | copy-start | bytes 772
  7.2 133.8 %all-gather.13.cloned.1.call-start = ((), (), s32[]{:S(2)}) async-start(), calls=%async_computation.4 | async-start | bytes 26738688 | tf_op jit(solution)/shard_map/all_gather | solution.py:183
  8.0 209.7 %all-gather.15.cloned.1.call-start = ((), (), s32[]{:S(2)}) async-start(), calls=%async_computation.5 | async-start | bytes 8912896 | tf_op jit(solution)/shard_map/all_gather | solution.py:200
  8.7 535.2 %all-gather.17.cloned.1.call-start = ((), (), s32[]{:S(2)}) async-start(), calls=%async_computation.6 | async-start | bytes 71303168 | tf_op jit(solution)/shard_map/all_gather | solution.py:211
  9.4 704.0 %all-gather.19.cloned.1.call-start = ((), (), s32[]{:S(2)}) async-start(), calls=%async_computation.7 | async-start | bytes 35651584 | tf_op jit(solution)/shard_map/all_gather | solution.py:221
  10.0 870.1 %all-gather.23.cloned.1.call-start = ((), (), s32[]{:S(2)}) async-start(), calls=%async_computation.9 | async-start | bytes 8912896 | tf_op jit(solution)/shard_map/all_gather | solution.py:261
  713.5 13.7 copy-start.8
  783.2 207.9 %all-gather.27.cloned.1.call-start = ((), (), s32[]{:S(2)}) async-start(), calls=%async_computation.11 | async-start | bytes 8912896 | tf_op jit(solution)/shard_map/all_gather | solution.py:258
  783.8 337.1 %all-gather.21.cloned.1.call-start = ((), (), s32[]{:S(2)}) async-start(), calls=%async_computation.8 | async-start | bytes 26738688 | tf_op jit(solution)/shard_map/all_gather | solution.py:260
  807.7 641.5 %all-gather.25.cloned.1.call-start = ((), (), s32[]{:S(2)}) async-start(), calls=%async_computation.10 | async-start | bytes 71303168 | tf_op jit(solution)/shard_map/all_gather | solution.py:259
  811.6 38.8 %copy-start.1 = (bf16[128,8192]{1,0:T(8,128)(2,1)S(1)}, bf16[128,8192]{1,0:T(8,128)(2,1)}, u32[]{:S(2)}) copy-start(bf16[128,8192]{1,0:T(8,128)(2,1)} %multiply_convert_fusion.2) | copy-start | bytes 6291460
  840.6 31.9 %all-to-all-start.1 = ((bf16[128,16,128]{0,2,1:T(8,128)(2,1)}), bf16[128,16,128]{0,2,1:T(8,128)(2,1)S(1)}, u32[]{:S(2)}, u32[]{:S(2)}) async-start(bf16[128,16,128]{0,2,1:T(8,128)(2,1)} %get-tuple-element.103), calls=%async_computation.1 | async-start | bytes 1048576 | tf_op jit(solution)/shard_map/all_to_all | solution.py:253
  850.4 28.4 %copy-start.7 = (bf16[128,2048]{1,0:T(8,128)(2,1)S(1)}, bf16[128,2048]{1,0:T(8,128)(2,1)}, u32[]{:S(2)}) copy-start(bf16[128,2048]{1,0:T(8,128)(2,1)} %fusion.10) | copy-start | bytes 1572868
  852.0 26.5 %copy-start.19 = (bf16[128,16,128]{0,2,1:T(8,128)(2,1)S(1)}, bf16[128,16,128]{0,2,1:T(8,128)(2,1)}, u32[]{:S(2)}) copy-start(bf16[128,16,128]{0,2,1:T(8,128)(2,1)} %all_to_all.73) | copy-start | bytes 1572868
  872.5 63.9 %all-to-all-start.3 = ((bf16[128,16,512]{2,0,1:T(8,128)(2,1)}), bf16[128,16,512]{2,0,1:T(8,128)(2,1)}, u32[]{:S(2)}, u32[]{:S(2)}) async-start(bf16[128,16,512]{2,0,1:T(8,128)(2,1)} %bitcast.120), calls=%async_computation.3 | async-start | bytes 4194304 | tf_op jit(solution)/shard_map/all_to_all | solution.py:250
  936.3 197.5 %all-to-all-start.2 = ((bf16[128,16,128]{2,0,1:T(8,128)(2,1)}), bf16[128,16,128]{2,0,1:T(8,128)(2,1)S(1)}, u32[]{:S(2)}, u32[]{:S(2)}) async-start(bf16[128,16,128]{2,0,1:T(8,128)(2,1)} %copy_bitcast_fusion.1), calls=%async_computation.2 | async-start | bytes 1048576 | tf_op jit(solution)/shard_map/all_to_all | solution.py:251
  955.7 718.0 %all-reduce.9.cloned.1.call-start = ((), (), s32[]{:S(2)}) async-start(), calls=%async_computation.12 | async-start | bytes 16777216 | tf_op jit(solution)/shard_map/psum | solution.py:279
  1475.3 70.2 %copy-start.17 = (f32[128,2048]{1,0:T(8,128)S(1)}, f32[128,2048]{1,0:T(8,128)}, u32[]{:S(2)}) copy-start(f32[128,2048]{1,0:T(8,128)} %get-tuple-element.109) | copy-start | bytes 3145732
  1475.3 70.2 %copy-start.21 = (bf16[128,2048]{1,0:T(8,128)(2,1)S(1)}, bf16[128,2048]{1,0:T(8,128)(2,1)}, u32[]{:S(2)}) copy-start(bf16[128,2048]{1,0:T(8,128)(2,1)} %copy.132) | copy-start | bytes 1572868
  1475.3 70.2 %copy-start.23 = (bf16[128,2048]{1,0:T(8,128)(2,1)S(1)}, bf16[128,2048]{1,0:T(8,128)(2,1)}, u32[]{:S(2)}) copy-start(bf16[128,2048]{1,0:T(8,128)(2,1)} %copy-done.22) | copy-start | bytes 1572868
  1475.4 70.2 %copy-start.25 = (bf16[128,2048]{1,0:T(8,128)(2,1)S(1)}, bf16[128,2048]{1,0:T(8,128)(2,1)}, u32[]{:S(2)}) copy-start(bf16[128,2048]{1,0:T(8,128)(2,1)} %copy-done.24) | copy-start | bytes 1572868
  (22 other events, 53.5 us)
Sparse Core Ops, SparseCore 0:
  9.6 131.3 all-gather.12
  143.2 74.4 all-gather.14
  219.3 324.6 all-gather.16
  545.4 168.0 all-gather.18
  783.3 94.6 all-gather.22
  880.1 111.0 all-gather.26
  993.3 127.5 all-gather.20
  1123.1 326.0 all-gather.24
  1475.5 198.1 all-reduce.8
where the time goes:
time: 1700 us; the launch traced here: 1690 us
  waiting for transfers between devices  1220 us (72%)
  matrix products  192 us (11%)
  blocking collectives  172 us (10%)
  other arithmetic  36.9 us (2%)
  starting transfers between devices  36.1 us (2%)
  local copies, waits for them, and re-layouts  17.3 us (1%)
    all_gather x1, waiting for transfers between devices, shards(): lax.all_gather(w_gate_up, 'shard', axis=0, tiled=True)  319 us
    all_gather x1, waiting for transfers between devices, shards(): lax.all_gather(d_gu_b, 'shard', axis=0, tiled=True)  315 us
    all_gather x1, waiting for transfers between devices, shards(): lax.all_gather(w_down, 'shard', axis=0, tiled=True)  134 us
    all_gather x1, waiting for transfers between devices, shards(): lax.all_gather(d_qkv_b, 'shard', axis=0, tiled=True)  120 us
    psum x1, waiting for transfers between devices, shards(): lax.psum(grad_qkv_own.astype(jnp.bfloat16), 'rep').astype(jnp.float32)  114 us
    dot_general x4, matrix products, contract_last(): lax.dot_general(left, right, (((1,), (1,)), ((), ())), preferred_element_...  72.1 us
    unnamed x1, blocking collectives  60.7 us
    all_gather x1, waiting for transfers between devices, shards(): lax.all_gather(w_out, 'shard', axis=0, tiled=True)  59.4 us
  transfers between devices with their start and end apart: 12, of which 10 were waited for; matrix products, arithmetic and copies ran while one was open for 8% of the time, Pallas kernels for 0%

commit v1 on v0

--- a/solution.py
+++ b/solution.py
@@ -205,12 +205,36 @@
     attn_norm, attn_hat, attn_scale = norm_forward(attn_raw, gain_attn)
     resid = tokens.astype(jnp.float32) + attn_norm
     resid_b = resid.astype(jnp.bfloat16)
+
+    def leaf_draft(local_values):
+        mesh_dim = "shard"
+        answer, ready, formed = (
+            lax.axis_size(mesh_dim),
+            lax.axis_index(mesh_dim),
+            local_values.shape[0],
+        )
+        blocks_here = tuple(((rr, (rr + 1) % answer) for rr in range(answer)))
+        pool = tuple(((rr, (rr - 1) % answer) for rr in range(answer)))
+        reached = jnp.zeros(
+            (*local_values.shape[:0], answer * formed, *local_values.shape[1:]), local_values.dtype
+        )
+        reached = lax.dynamic_update_slice_in_dim(reached, local_values, ready * formed, axis=0)
+        step_out = res = local_values
+        r2 = answer // 2
+        for dd in [*range(1, r2 + 1)]:
+            step_out = lax.ppermute(step_out, mesh_dim, blocks_here)
+            reached = lax.dynamic_update_slice_in_dim(
+                reached, step_out, (ready - dd) % answer * formed, axis=0
+            )
+            if dd < answer - r2:
+                res = lax.ppermute(res, mesh_dim, pool)
+                reached = lax.dynamic_update_slice_in_dim(
+                    reached, res, (ready + dd) % answer * formed, axis=0
+                )
+        return reached
+
     gate_up, mlp_gain_full = fold_gain(
-        resid_b,
-        (
-            lax.all_gather(w_gate_up, "shard", axis=0, tiled=True),
-            lax.all_gather(mlp_gain, "shard", axis=0, tiled=True),
-        ),
+        resid_b, (leaf_draft(w_gate_up), lax.all_gather(mlp_gain, "shard", axis=0, tiled=True))
     )
     gain_mlp = mlp_gain_full.astype(jnp.float32)
     gate_raw = gate_up[:, :ff_width]

time: 1700 us -> 2320 us (1.36)
  starting transfers between devices: 36.1 us -> 603 us
  waiting for transfers between devices: 1220 us -> 1040 us
  blocking collectives: 172 us -> 329 us
  local copies, waits for them, and re-layouts: 17.3 us -> 94 us
    ppermute x0 -> x15, starting transfers between devices: none -> 572 us  [the longest x8 562 us: leaf_draft(): step_out = lax.ppermute(step_out, mesh_dim, blocks_here)]
    ppermute x0 -> x15, waiting for transfers between devices: none -> 432 us  [the longest x8 366 us: leaf_draft(): step_out = lax.ppermute(step_out, mesh_dim, blocks_here)]
    all_gather x1, waiting for transfers between devices: 319 us -> 0.01 us  [shards(): lax.all_gather(w_gate_up, 'shard', axis=0, tiled=True)]
    all_gather x1, waiting for transfers between devices: 134 us -> 0.01 us  [shards(): lax.all_gather(w_down, 'shard', axis=0, tiled=True)]
    all_gather x1, blocking collectives: 23.4 us -> 145 us  [shards(): lax.all_gather(q_gain, 'shard', axis=0, tiled=True)]
    all_gather x1, waiting for transfers between devices: 59.4 us -> 0.01 us  [shards(): lax.all_gather(w_out, 'shard', axis=0, tiled=True)]
    dynamic_update_slice x0 -> x16, local copies, waits for them, and re-layouts: none -> 53 us  [the longest x8 27.6 us: leaf_draft(): lax.dynamic_update_slice_in_dim(reached, step_out, (ready - dd) % answer...]
    all_gather x1, waiting for transfers between devices: 51.1 us -> 0.01 us  [shards(): lax.all_gather(w_qkv, 'shard', axis=0, tiled=True)]
  transfers between devices with their start and end apart: 12 -> 27, of which waited for: 10 -> 12; matrix products, arithmetic and copies ran while one was open for 8% -> 12% of each run, Pallas kernels for 0% -> 0%
where the time goes in v1:
time: 2320 us
  waiting for transfers between devices  1040 us (45%)
  starting transfers between devices  603 us (26%)
  blocking collectives  329 us (14%)
  matrix products  193 us (8%)
  local copies, waits for them, and re-layouts  94 us (4%)
  other arithmetic  37 us (2%)
    ppermute x8, starting transfers between devices, leaf_draft(): step_out = lax.ppermute(step_out, mesh_dim, blocks_here)  562 us
    ppermute x8, waiting for transfers between devices, leaf_draft(): step_out = lax.ppermute(step_out, mesh_dim, blocks_here)  366 us
    all_gather x1, waiting for transfers between devices, shards(): lax.all_gather(d_gu_b, 'shard', axis=0, tiled=True)  320 us
    all_gather x1, blocking collectives, shards(): lax.all_gather(q_gain, 'shard', axis=0, tiled=True)  145 us
    psum x1, waiting for transfers between devices, shards(): lax.psum(grad_qkv_own.astype(jnp.bfloat16), 'rep').astype(jnp.float32)  114 us
    all_gather x1, waiting for transfers between devices, shards(): lax.all_gather(d_qkv_b, 'shard', axis=0, tiled=True)  103 us
    dot_general x4, matrix products, contract_last(): lax.dot_general(left, right, (((1,), (1,)), ((), ())), preferred_element_...  73 us
    ppermute x7, waiting for transfers between devices, leaf_draft(): res = lax.ppermute(res, mesh_dim, pool)  65.8 us
  transfers between devices with their start and end apart: 27, of which 12 were waited for; matrix products, arithmetic and copies ran while one was open for 12% of the time, Pallas kernels for 0%

profile of v1, /device:TPU:0, one launch (start us, length us, event | category | flops | bytes accessed | tf_op | source)
XLA Modules:
  0.0 2316.6 jit_solution(10462330722076007763)
XLA Ops:
  15.6 84.3 %collective-permute-done = bf16[128,16384]{1,0:T(8,128)(2,1)S(1)} collective-permute-done((bf16[128,16384]{1,0:T(8,128)(2,1)}, bf16[128,16384]{1,0:T(8,128)(2,1)S(1)}, u32[]{:S(2)}, u32[]{:S(2)}) %collective-permute-start) | collective-permute-done | bytes 4194336 | tf_op jit(solution)/shard_map/ppermute | solution.py:225
  101.9 133.2 %collective-permute-start.2 = (bf16[128,16384]{1,0:T(8,128)(2,1)S(1)}, bf16[128,16384]{1,0:T(8,128)(2,1)}, u32[]{:S(2)}, u32[]{:S(2)}) collective-permute-start(bf16[128,16384]{1,0:T(8,128)(2,1)S(1)} %collective-permute-done), channel_id=1, source_target_pairs={{0,1},{1,2},{2,3},{3,4},{4,5},{5,6},{6,7},{7,8},{8,9},{9,10},{10,1... | collective-permute-start | bytes 12582920 | tf_op jit(solution)/shard_map/ppermute | solution.py:225
  242.6 114.0 %collective-permute-start.4 = (bf16[128,16384]{1,0:T(8,128)(2,1)}, bf16[128,16384]{1,0:T(8,128)(2,1)}, u32[]{:S(2)}, u32[]{:S(2)}) collective-permute-start(bf16[128,16384]{1,0:T(8,128)(2,1)} %collective-permute-done.2), channel_id=1, source_target_pairs={{0,1},{1,2},{2,3},{3,4},{4,5},{5,6},{6,7},{7,8},{8,9},{9,10},{10,1... | collective-permute-start | bytes 12582920 | tf_op jit(solution)/shard_map/ppermute | solution.py:225
  357.3 21.7 broadcast_in_dim.27
  381.3 29.2 %collective-permute-start.6 = (bf16[128,16384]{1,0:T(8,128)(2,1)}, bf16[128,16384]{1,0:T(8,128)(2,1)}, u32[]{:S(2)}, u32[]{:S(2)}) collective-permute-start(bf16[128,16384]{1,0:T(8,128)(2,1)} %collective-permute-done.4), channel_id=1, source_target_pairs={{0,1},{1,2},{2,3},{3,4},{4,5},{5,6},{6,7},{7,8},{8,9},{9,10},{10,1... | collective-permute-start | bytes 12582920 | tf_op jit(solution)/shard_map/ppermute | solution.py:225
  410.6 145.0 %all-gather = bf16[16,1,128]{2,1,0:T(2,128)(2,1)S(1)} all-gather(bf16[1,1,128]{2,1,0:T(2,128)(2,1)S(1)} %bitcast.143), channel_id=1, replica_groups=mesh['rep'=2,'shard'=16] {'shard'}, dimensions={0}, use_global_device_ids=true | all-gather | bytes 4352 | tf_op jit(solution)/shard_map/all_gather | solution.py:184
  631.4 65.8 %collective-permute-done.7 = bf16[128,16384]{1,0:T(8,128)(2,1)S(1)} collective-permute-done((bf16[128,16384]{1,0:T(8,128)(2,1)}, bf16[128,16384]{1,0:T(8,128)(2,1)S(1)}, u32[]{:S(2)}, u32[]{:S(2)}) %collective-permute-start.7) | collective-permute-done | bytes 4194336 | tf_op jit(solution)/shard_map/ppermute | solution.py:230
  713.2 105.7 %collective-permute-start.10 = (bf16[128,16384]{1,0:T(8,128)(2,1)S(1)}, bf16[128,16384]{1,0:T(8,128)(2,1)S(1)}, u32[]{:S(2)}, u32[]{:S(2)}) collective-permute-start(bf16[128,16384]{1,0:T(8,128)(2,1)S(1)} %collective-permute-done.8), channel_id=1, source_target_pairs={{0,1},{1,2},{2,3},{3,4},{4,5},{5,6},{6,7},{7,8},{8,9},{9,10},{10,1... | collective-permute-start | bytes 12582920 | tf_op jit(solution)/shard_map/ppermute | solution.py:225
  830.2 102.3 %collective-permute-done.10 = bf16[128,16384]{1,0:T(8,128)(2,1)S(1)} collective-permute-done((bf16[128,16384]{1,0:T(8,128)(2,1)S(1)}, bf16[128,16384]{1,0:T(8,128)(2,1)S(1)}, u32[]{:S(2)}, u32[]{:S(2)}) %collective-permute-start.10) | collective-permute-done | bytes 4194336 | tf_op jit(solution)/shard_map/ppermute | solution.py:225
  932.5 89.6 %collective-permute-start.12 = (bf16[128,16384]{1,0:T(8,128)(2,1)S(1)}, bf16[128,16384]{1,0:T(8,128)(2,1)S(1)}, u32[]{:S(2)}, u32[]{:S(2)}) collective-permute-start(bf16[128,16384]{1,0:T(8,128)(2,1)S(1)} %collective-permute-done.10), channel_id=1, source_target_pairs={{0,1},{1,2},{2,3},{3,4},{4,5},{5,6},{6,7},{7,8},{8,9},{9,10},{10,1... | collective-permute-start | bytes 12582920 | tf_op jit(solution)/shard_map/ppermute | solution.py:225
  1028.9 49.7 %collective-permute-done.12 = bf16[128,16384]{1,0:T(8,128)(2,1)S(1)} collective-permute-done((bf16[128,16384]{1,0:T(8,128)(2,1)S(1)}, bf16[128,16384]{1,0:T(8,128)(2,1)S(1)}, u32[]{:S(2)}, u32[]{:S(2)}) %collective-permute-start.12) | collective-permute-done | bytes 4194336 | tf_op jit(solution)/shard_map/ppermute | solution.py:225
  1078.6 89.3 %collective-permute-start.14 = (bf16[128,16384]{1,0:T(8,128)(2,1)S(1)}, bf16[128,16384]{1,0:T(8,128)(2,1)S(1)}, u32[]{:S(2)}, u32[]{:S(2)}) collective-permute-start(bf16[128,16384]{1,0:T(8,128)(2,1)S(1)} %collective-permute-done.12), channel_id=1, source_target_pairs={{0,1},{1,2},{2,3},{3,4},{4,5},{5,6},{6,7},{7,8},{8,9},{9,10},{10,1... | collective-permute-start | bytes 12582920 | tf_op jit(solution)/shard_map/ppermute | solution.py:225
  1174.9 115.7 %collective-permute-done.14 = bf16[128,16384]{1,0:T(8,128)(2,1)S(1)} collective-permute-done((bf16[128,16384]{1,0:T(8,128)(2,1)S(1)}, bf16[128,16384]{1,0:T(8,128)(2,1)S(1)}, u32[]{:S(2)}, u32[]{:S(2)}) %collective-permute-start.14) | collective-permute-done | bytes 4194336 | tf_op jit(solution)/shard_map/ppermute | solution.py:225
  1317.5 27.9 %fusion.28 = f32[128,16384]{1,0:T(8,128)} fusion(bf16[128,2048]{1,0:T(8,128)(2,1)} %fusion.10, bf16[2048,16384]{1,0:T(8,128)(2,1)} %constant_dynamic-update-slice_fusion), kind=kOutput, calls=%fused_computation.121 | convolution fusion | flops 8589934592 | bytes 76021760 | tf_op jit(solution)/shard_map/dot_general | solution.py:138
  1367.7 20.1 multiply_convert_fusion.1
  1387.8 31.0 %multiply_reduce_fusion.1 = (bf16[2048]{0:T(1024)(128)(2,1)S(1)}, f32[128]{0:T(128)S(1)}, f32[128,2048]{1,0:T(8,128)}) fusion(f32[128,2048]{1,0:T(8,128)} %copy-done.2, f32[128]{0:T(128)S(1)} %add_rsqrt_fusion.1, f32[2048]{0:T(1024)S(1)} %bitcast.131, bf16[2048,16384]{1,0:T(8,128)(2,1)} %all-gather.19.cloned.1.call-done, ...), kind=kOutput, calls=%fused_computation.36 | convolution fusion | flops 8600680448 | bytes 73938432 | tf_op jit(solution)/shard_map/dot_general | solution.py:64
  1451.5 62.4 %all_to_all.73 = bf16[128,16,128]{0,2,1:T(8,128)(2,1)} all-to-all(bf16[128,16,128]{0,2,1:T(8,128)(2,1)S(1)} %bitcast.127), channel_id=1, replica_groups=mesh['rep'=2,'shard'=16] {'shard'}, dimensions={1} | all-to-all | bytes 1048576 | tf_op jit(solution)/shard_map/all_to_all | solution.py:276
  1522.5 21.3 all-to-all-done.1
  1555.2 52.3 %all-to-all-done.3 = bf16[128,16,512]{2,0,1:T(8,128)(2,1)} async-done(((bf16[128,16,512]{2,0,1:T(8,128)(2,1)}), bf16[128,16,512]{2,0,1:T(8,128)(2,1)}, u32[]{:S(2)}, u32[]{:S(2)}) %all-to-all-start.3) | async-done | bytes 2097184 | tf_op jit(solution)/shard_map/all_to_all | solution.py:274
  1636.9 102.7 %all-gather.21.cloned.1.call-done = bf16[2048,6144]{1,0:T(8,128)(2,1)} async-done(((bf16[128,6144]{1,0:T(8,128)(2,1)}), bf16[2048,6144]{1,0:T(8,128)(2,1)}) %all-gather.21.cloned.1.call-update) | async-done | bytes 25165840 | tf_op jit(solution)/shard_map/all_gather | solution.py:284
  1752.8 320.0 %all-gather.25.cloned.1.call-done = bf16[2048,16384]{1,0:T(8,128)(2,1)} async-done(((bf16[128,16384]{1,0:T(8,128)(2,1)}), bf16[2048,16384]{1,0:T(8,128)(2,1)}) %all-gather.25.cloned.1.call-update) | async-done | bytes 67108880 | tf_op jit(solution)/shard_map/all_gather | solution.py:283
  2072.8 26.2 %convolution_convert_fusion = bf16[128,16384]{1,0:T(8,128)(2,1)} fusion(bf16[2048,128]{1,0:T(8,128)(2,1)S(1)} %bitcast.124, bf16[2048,16384]{1,0:T(8,128)(2,1)} %all-gather.25.cloned.1.call-done), kind=kOutput, calls=%fused_computation | convolution fusion | flops 8592031744 | bytes 71827456 | tf_op jit(solution)/shard_map/dot_general | solution.py:70
  2100.8 60.7 %all-reduce.4 = (bf16[2048]{0:T(1024)(128)(2,1)S(1)}, bf16[2048]{0:T(1024)(128)(2,1)S(1)}, bf16[2048]{0:T(1024)(128)(2,1)S(1)}, bf16[2048]{0:T(1024)(128)(2,1)S(1)}) all-reduce(bf16[2048]{0:T(1024)(128)(2,1)S(1)} %get-tuple-element.55, ...), channel_id=2, replica_groups=mesh['rep'=2,'shard'=16] {'shard'}, use_global_device_ids=true, to_apply=%region_17.18.clone | all-reduce | flops 8192 | bytes 32768
  2183.7 113.6 %all-reduce.9.cloned.1.call-done = (bf16[128,6144]{0,1:T(8,128)(2,1)}, bf16[128,2048]{1,0:T(8,128)(2,1)}, bf16[128,16384]{1,0:T(8,128)(2,1)}, bf16[512,2048]{1,0:T(8,128)(2,1)}) async-done(((bf16[128,6144]{0,1:T(8,128)(2,1)}, bf16[128,2048]{1,0:T(8,128)(2,1)}, bf16[128,16384]{1,0:T(8,128)(2,1)}, bf16[512,2048]{1,0:T(8,128)(2,1)}), (bf16[128,6144]{0,1:T(8,128)(2,1)}, bf16[128,2048]{1,0:T(8,128)(2,1)}, ...) | async-done | bytes 8388624 | tf_op jit(solution)/shard_map/psum | solution.py:303
  (214 shorter events, 317.5 us)
Async XLA Ops:
  7.2 1285.6 %all-gather.13.cloned.1.call-start = ((), (), s32[]{:S(2)}) async-start(), calls=%async_computation.4 | async-start | bytes 26738688 | tf_op jit(solution)/shard_map/all_gather | solution.py:183
  7.9 1302.2 %all-gather.15.cloned.1.call-start = ((), (), s32[]{:S(2)}) async-start(), calls=%async_computation.5 | async-start | bytes 8912896 | tf_op jit(solution)/shard_map/all_gather | solution.py:200
  8.7 1342.9 %all-gather.17.cloned.1.call-start = ((), (), s32[]{:S(2)}) async-start(), calls=%async_computation.6 | async-start | bytes 35651584 | tf_op jit(solution)/shard_map/all_gather | solution.py:245
  9.4 1378.4 %all-gather.19.cloned.1.call-start = ((), (), s32[]{:S(2)}) async-start(), calls=%async_computation.7 | async-start | bytes 71303168 | tf_op jit(solution)/shard_map/all_gather | solution.py:256
  10.0 1611.5 %all-gather.27.cloned.1.call-start = ((), (), s32[]{:S(2)}) async-start(), calls=%async_computation.11 | async-start | bytes 8912896 | tf_op jit(solution)/shard_map/all_gather | solution.py:282
  10.0 89.9 %collective-permute-start = (bf16[128,16384]{1,0:T(8,128)(2,1)}, bf16[128,16384]{1,0:T(8,128)(2,1)S(1)}, u32[]{:S(2)}, u32[]{:S(2)}) collective-permute-start(bf16[128,16384]{1,0:T(8,128)(2,1)} %param.16), channel_id=1, source_target_pairs={{0,1},{1,2},{2,3},{3,4},{4,5},{5,6},{6,7},{7,8},{8,9},{9,10},{10,1... | collective-permute-start | bytes 12582920 | tf_op jit(solution)/shard_map/ppermute | solution.py:225
  10.6 224.5 %collective-permute-start.1 = (bf16[128,16384]{1,0:T(8,128)(2,1)}, bf16[128,16384]{1,0:T(8,128)(2,1)}, u32[]{:S(2)}, u32[]{:S(2)}) collective-permute-start(bf16[128,16384]{1,0:T(8,128)(2,1)} %param.16), channel_id=1, source_target_pairs={{0,15},{1,0},{2,1},{3,2},{4,3},{5,4},{6,5},{7,6},{8,7},{9,8},{10,9... | collective-permute-start | bytes 12582920 | tf_op jit(solution)/shard_map/ppermute | solution.py:230
  101.9 140.7 %collective-permute-start.2 = (bf16[128,16384]{1,0:T(8,128)(2,1)S(1)}, bf16[128,16384]{1,0:T(8,128)(2,1)}, u32[]{:S(2)}, u32[]{:S(2)}) collective-permute-start(bf16[128,16384]{1,0:T(8,128)(2,1)S(1)} %collective-permute-done), channel_id=1, source_target_pairs={{0,1},{1,2},{2,3},{3,4},{4,5},{5,6},{6,7},{7,8},{8,9},{9,10},{10,1... | collective-permute-start | bytes 12582920 | tf_op jit(solution)/shard_map/ppermute | solution.py:225
  235.1 122.1 %collective-permute-start.3 = (bf16[128,16384]{1,0:T(8,128)(2,1)}, bf16[128,16384]{1,0:T(8,128)(2,1)}, u32[]{:S(2)}, u32[]{:S(2)}) collective-permute-start(bf16[128,16384]{1,0:T(8,128)(2,1)} %collective-permute-done.1), channel_id=1, source_target_pairs={{0,15},{1,0},{2,1},{3,2},{4,3},{5,4},{6,5},{7,6},{8,7},{9,8},{10,9... | collective-permute-start | bytes 12582920 | tf_op jit(solution)/shard_map/ppermute | solution.py:230
  242.6 138.7 %collective-permute-start.4 = (bf16[128,16384]{1,0:T(8,128)(2,1)}, bf16[128,16384]{1,0:T(8,128)(2,1)}, u32[]{:S(2)}, u32[]{:S(2)}) collective-permute-start(bf16[128,16384]{1,0:T(8,128)(2,1)} %collective-permute-done.2), channel_id=1, source_target_pairs={{0,1},{1,2},{2,3},{3,4},{4,5},{5,6},{6,7},{7,8},{8,9},{9,10},{10,1... | collective-permute-start | bytes 12582920 | tf_op jit(solution)/shard_map/ppermute | solution.py:225
  357.3 259.4 %collective-permute-start.5 = (bf16[128,16384]{1,0:T(8,128)(2,1)}, bf16[128,16384]{1,0:T(8,128)(2,1)}, u32[]{:S(2)}, u32[]{:S(2)}) collective-permute-start(bf16[128,16384]{1,0:T(8,128)(2,1)} %collective-permute-done.3), channel_id=1, source_target_pairs={{0,15},{1,0},{2,1},{3,2},{4,3},{5,4},{6,5},{7,6},{8,7},{9,8},{10,9... | collective-permute-start | bytes 12582920 | tf_op jit(solution)/shard_map/ppermute | solution.py:230
  381.3 240.9 %collective-permute-start.6 = (bf16[128,16384]{1,0:T(8,128)(2,1)}, bf16[128,16384]{1,0:T(8,128)(2,1)}, u32[]{:S(2)}, u32[]{:S(2)}) collective-permute-start(bf16[128,16384]{1,0:T(8,128)(2,1)} %collective-permute-done.4), channel_id=1, source_target_pairs={{0,1},{1,2},{2,3},{3,4},{4,5},{5,6},{6,7},{7,8},{8,9},{9,10},{10,1... | collective-permute-start | bytes 12582920 | tf_op jit(solution)/shard_map/ppermute | solution.py:225
  622.2 91.0 %collective-permute-start.8 = (bf16[128,16384]{1,0:T(8,128)(2,1)}, bf16[128,16384]{1,0:T(8,128)(2,1)S(1)}, u32[]{:S(2)}, u32[]{:S(2)}) collective-permute-start(bf16[128,16384]{1,0:T(8,128)(2,1)} %collective-permute-done.6), channel_id=1, source_target_pairs={{0,1},{1,2},{2,3},{3,4},{4,5},{5,6},{6,7},{7,8},{8,9},{9,10},{10,1... | collective-permute-start | bytes 12582920 | tf_op jit(solution)/shard_map/ppermute | solution.py:225
  697.2 130.7 %collective-permute-start.9 = (bf16[128,16384]{1,0:T(8,128)(2,1)S(1)}, bf16[128,16384]{1,0:T(8,128)(2,1)S(1)}, u32[]{:S(2)}, u32[]{:S(2)}) collective-permute-start(bf16[128,16384]{1,0:T(8,128)(2,1)S(1)} %collective-permute-done.7), channel_id=1, source_target_pairs={{0,15},{1,0},{2,1},{3,2},{4,3},{5,4},{6,5},{7,6},{8,7},{9,8},{10,9... | collective-permute-start | bytes 12582920 | tf_op jit(solution)/shard_map/ppermute | solution.py:230
  713.2 219.3 %collective-permute-start.10 = (bf16[128,16384]{1,0:T(8,128)(2,1)S(1)}, bf16[128,16384]{1,0:T(8,128)(2,1)S(1)}, u32[]{:S(2)}, u32[]{:S(2)}) collective-permute-start(bf16[128,16384]{1,0:T(8,128)(2,1)S(1)} %collective-permute-done.8), channel_id=1, source_target_pairs={{0,1},{1,2},{2,3},{3,4},{4,5},{5,6},{6,7},{7,8},{8,9},{9,10},{10,1... | collective-permute-start | bytes 12582920 | tf_op jit(solution)/shard_map/ppermute | solution.py:225
  827.9 198.7 %collective-permute-start.11 = (bf16[128,16384]{1,0:T(8,128)(2,1)S(1)}, bf16[128,16384]{1,0:T(8,128)(2,1)S(1)}, u32[]{:S(2)}, u32[]{:S(2)}) collective-permute-start(bf16[128,16384]{1,0:T(8,128)(2,1)S(1)} %collective-permute-done.9), channel_id=1, source_target_pairs={{0,15},{1,0},{2,1},{3,2},{4,3},{5,4},{6,5},{7,6},{8,7},{9,8},{10,9... | collective-permute-start | bytes 12582920 | tf_op jit(solution)/shard_map/ppermute | solution.py:230
  932.5 146.1 %collective-permute-start.12 = (bf16[128,16384]{1,0:T(8,128)(2,1)S(1)}, bf16[128,16384]{1,0:T(8,128)(2,1)S(1)}, u32[]{:S(2)}, u32[]{:S(2)}) collective-permute-start(bf16[128,16384]{1,0:T(8,128)(2,1)S(1)} %collective-permute-done.10), channel_id=1, source_target_pairs={{0,1},{1,2},{2,3},{3,4},{4,5},{5,6},{6,7},{7,8},{8,9},{9,10},{10,1... | collective-permute-start | bytes 12582920 | tf_op jit(solution)/shard_map/ppermute | solution.py:225
  1026.6 145.9 %collective-permute-start.13 = (bf16[128,16384]{1,0:T(8,128)(2,1)S(1)}, bf16[128,16384]{1,0:T(8,128)(2,1)S(1)}, u32[]{:S(2)}, u32[]{:S(2)}) collective-permute-start(bf16[128,16384]{1,0:T(8,128)(2,1)S(1)} %collective-permute-done.11), channel_id=1, source_target_pairs={{0,15},{1,0},{2,1},{3,2},{4,3},{5,4},{6,5},{7,6},{8,7},{9,8},{10,9... | collective-permute-start | bytes 12582920 | tf_op jit(solution)/shard_map/ppermute | solution.py:230
  1078.6 211.9 %collective-permute-start.14 = (bf16[128,16384]{1,0:T(8,128)(2,1)S(1)}, bf16[128,16384]{1,0:T(8,128)(2,1)S(1)}, u32[]{:S(2)}, u32[]{:S(2)}) collective-permute-start(bf16[128,16384]{1,0:T(8,128)(2,1)S(1)} %collective-permute-done.12), channel_id=1, source_target_pairs={{0,1},{1,2},{2,3},{3,4},{4,5},{5,6},{6,7},{7,8},{8,9},{9,10},{10,1... | collective-permute-start | bytes 12582920 | tf_op jit(solution)/shard_map/ppermute | solution.py:225
  1367.7 263.8 %all-gather.23.cloned.1.call-start = ((), (), s32[]{:S(2)}) async-start(), calls=%async_computation.9 | async-start | bytes 8912896 | tf_op jit(solution)/shard_map/all_gather | solution.py:285
  1422.3 317.4 %all-gather.21.cloned.1.call-start = ((), (), s32[]{:S(2)}) async-start(), calls=%async_computation.8 | async-start | bytes 26738688 | tf_op jit(solution)/shard_map/all_gather | solution.py:284
  1446.1 626.7 %all-gather.25.cloned.1.call-start = ((), (), s32[]{:S(2)}) async-start(), calls=%async_computation.10 | async-start | bytes 71303168 | tf_op jit(solution)/shard_map/all_gather | solution.py:283
  1607.6 145.2 %all-to-all-start.2 = ((bf16[128,16,128]{2,0,1:T(8,128)(2,1)}), bf16[128,16,128]{2,0,1:T(8,128)(2,1)S(1)}, u32[]{:S(2)}, u32[]{:S(2)}) async-start(bf16[128,16,128]{2,0,1:T(8,128)(2,1)} %copy_bitcast_fusion.1), calls=%async_computation.2 | async-start | bytes 1048576 | tf_op jit(solution)/shard_map/all_to_all | solution.py:275
  1621.2 676.1 %all-reduce.9.cloned.1.call-start = ((), (), s32[]{:S(2)}) async-start(), calls=%async_computation.12 | async-start | bytes 16777216 | tf_op jit(solution)/shard_map/psum | solution.py:303
  (39 other events, 1644.5 us)
Sparse Core Ops, SparseCore 0:
  9.6 332.8 all-gather.12
  344.6 128.5 all-gather.14
  474.8 273.9 all-gather.16
  750.3 597.2 all-gather.18
  1367.8 108.9 all-gather.26
  1478.8 122.7 all-gather.22
  1603.8 135.7 all-gather.20
  1741.8 330.9 all-gather.24
  2099.1 198.1 all-reduce.8
